TPU v7x, 32 devices: a whole 2x2x4 slice. The times are simulated.
32 devices in a mesh: lat: 16 (over z, y, core), lon: 2 (over x).
Axes of the slice: x: 2, y: 2, z: 4, core: 2. Of those that a mesh axis runs over, the one named last changes fastest.
Arguments:
- features: bfloat16 [256, 128, 512], P('lat', 'lon'), may hold values from -6 to 6
- upstream: bfloat16 [256, 128, 512], P('lat', 'lon'), may hold values from -6 to 6
- kernel: bfloat16 [4608, 512], replicated, may hold values from -0.09375 to 0.09375
Outputs:
- input_grad: bfloat16 [256, 128, 512], P('lat', 'lon')
- direction: float32 [4608, 512], P('lat')
- perturbed: float32 [4608, 512], P('lat')
All inputs are finite; a program needn't handle non-finite values.
Results may differ from a plain program's by a relative error of at most 0.0032.
Values may be sent and summed in bfloat16 or wider, within the bound.
A program may use at most 128 MiB of HBM per device.

v0:
```python
import jax
import jax.numpy as jnp
from jax import lax
from jax.sharding import PartitionSpec as P


def padded_2(block, sides, width, periodic):
    for axis, dim in sides:
        count = lax.axis_size(axis)
        forward = [(i, i + 1) for i in range(count - 1)]
        if periodic:
            forward.append((count - 1, 0))
        backward = [(target, source) for source, target in forward]
        low = lax.ppermute(
            lax.slice_in_dim(block, block.shape[dim] - width, None, axis=dim), axis, forward
        )
        high = lax.ppermute(lax.slice_in_dim(block, 0, width, axis=dim), axis, backward)
        block = jnp.concatenate([low, block, high], axis=dim)
    return block


def convolve(padded, kernel, height, breadth):
    channels = kernel.shape[1]
    total = jnp.zeros((height, breadth, channels), jnp.float32)
    for a in range(3):
        for b in range(3):
            t = 3 * a + b
            total = total + jnp.dot(
                padded[a : a + height, b : b + breadth],
                kernel[t * channels : (t + 1) * channels],
                preferred_element_type=jnp.float32,
            )
    return total


def spread(padded, kernel, height, breadth):
    channels = kernel.shape[1]
    total = jnp.zeros((height, breadth, channels), jnp.float32)
    for a in range(3):
        for b in range(3):
            t = 3 * a + b
            piece = padded[2 - a : 2 - a + height, 2 - b : 2 - b + breadth]
            total = total + lax.dot_general(
                piece,
                kernel[t * channels : (t + 1) * channels],
                (((2,), (1,)), ((), ())),
                preferred_element_type=jnp.float32,
            )
    return total


def weight_terms(padded, slope, height, breadth):
    blocks = []
    for a in range(3):
        for b in range(3):
            blocks.append(
                lax.dot_general(
                    padded[a : a + height, b : b + breadth],
                    slope,
                    (((0, 1), (0, 1)), ((), ())),
                    preferred_element_type=jnp.float32,
                )
            )
    return jnp.concatenate(blocks, axis=0)


def gated(upstream, z):
    sig = jax.nn.sigmoid(z)
    return upstream.astype(jnp.float32) * sig * (1.0 + z * (1.0 - sig))


def shards(features, upstream, kernel):
    height, breadth, channels = features.shape
    wide_cols = padded_2(features, (("lon", 1),), 1, True)
    padded_x = padded_2(wide_cols, (("lat", 0),), 1, False)
    z = convolve(padded_x, kernel, height, breadth)
    slope = gated(upstream, z).astype(jnp.bfloat16)
    slope_cols = padded_2(slope, (("lon", 1),), 1, True)
    padded_slope = padded_2(slope_cols, (("lat", 0),), 1, False)
    back = upstream.astype(jnp.float32) + spread(padded_slope, kernel, height, breadth)
    input_grad = back.astype(jnp.bfloat16)
    local_grad = weight_terms(padded_x, slope, height, breadth)
    row_block = lax.psum_scatter(local_grad, "lat", scatter_dimension=0, tiled=True)
    summed = lax.psum(row_block, "lon")
    total = lax.psum(jnp.sum(summed * summed), "lat")
    count = 9.0 * channels * channels
    direction = summed / jnp.sqrt(total / count + 1e-06)
    block_rows = summed.shape[0]
    start = lax.axis_index("lat") * block_rows
    own_kernel = lax.dynamic_slice_in_dim(kernel, start, block_rows, 0)
    perturbed = own_kernel.astype(jnp.float32) + 0.05 / jnp.sqrt(count) * direction
    return (input_grad, direction, perturbed)


def solution(mesh):
    return jax.shard_map(
        shards,
        mesh=mesh,
        in_specs=(P("lat", "lon", None), P("lat", "lon", None), P()),
        out_specs=(P("lat", "lon", None), P("lat", None), P("lat", None)),
        check_vma=False,
    )
```

profile of v0, /device:TPU:0, one launch (start us, length us, event | category | flops | bytes accessed | tf_op | source)
XLA Modules:
  0.0 243.8 jit_solution(826851262055394935)
XLA Ops:
  8.3 3.0 %collective-permute-start = (bf16[16,1,512]{2,1,0:T(2,128)(2,1)S(1)}, bf16[16,1,512]{2,1,0:T(2,128)(2,1)S(1)}, u32[]{:S(2)}, u32[]{:S(2)}) collective-permute-start(bf16[16,1,512]{2,1,0:T(2,128)(2,1)S(1)} %get-tuple-element.15), channel_id=1, source_target_pairs={{0,1},{1,0},{2,3},{3,2},{4,5},{5,4},{6,7},{7,6},{8,9},{9,8},{10,11... | collective-permute-start | bytes 49160 | tf_op jit(solution)/shard_map/ppermute | solution.py:14
  11.4 2.1 fusion.62
  13.5 1.8 collective-permute-done.1
  15.3 1.6 collective-permute-start.2
  16.9 1.3 collective-permute-start.3
  18.2 1.8 fusion.50
  26.6 1.8 fusion.1
  28.4 1.7 fusion.11
  30.1 1.7 fusion.10
  31.8 1.7 fusion.9
  33.6 1.8 fusion.8
  35.3 1.7 fusion.7
  37.1 1.8 fusion.6
  38.8 1.7 fusion.5
  40.5 1.8 fusion.4
  42.3 1.8 fusion.3
  44.9 1.5 collective-permute-start.4
  46.4 1.8 fusion.60
  50.1 4.4 %collective-permute-start.7 = (bf16[1,66,512]{2,1,0:T(8,128)(2,1)S(1)}, bf16[1,66,512]{2,1,0:T(8,128)(2,1)S(1)}, u32[]{:S(2)}, u32[]{:S(2)}) collective-permute-start(bf16[1,66,512]{2,1,0:T(8,128)(2,1)S(1)} %get-tuple-element.8), channel_id=1, source_target_pairs={{0,2},{2,4},{4,6},{6,8},{8,10},{10,12},{12,14},{14,16},{16,18},{18... | collective-permute-start | bytes 202760 | tf_op jit(solution)/shard_map/ppermute | solution.py:14
  54.5 3.3 %fusion.22 = f32[16,64,512]{2,1,0:T(8,128)} fusion(bf16[16,1,512]{2,1,0:T(2,128)(2,1)S(1)} %collective-permute-done.5, bf16[16,64,512]{2,1,0:T(8,128)(2,1)S(1)} %fusion.1, bf16[4608,512]{1,0:T(8,128)(2,1)} %param.5), kind=kOutput, calls=%fused_computation.37 | convolution fusion | flops 538968064 | bytes 3686400 | tf_op jit(solution)/shard_map/dot_general | solution.py:43
  57.9 3.1 %fusion.20 = f32[16,64,512]{2,1,0:T(8,128)} fusion(bf16[16,64,512]{2,1,0:T(8,128)(2,1)S(1)} %fusion.1, bf16[16,1,512]{2,1,0:T(2,128)(2,1)S(1)} %collective-permute-done.4, bf16[4608,512]{1,0:T(8,128)(2,1)} %param.5), kind=kOutput, calls=%fused_computation.34 | convolution fusion | flops 538968064 | bytes 3686400 | tf_op jit(solution)/shard_map/dot_general | solution.py:43
  61.8 3.6 %fusion.16 = f32[16,64,512]{2,1,0:T(8,128)} fusion(bf16[17,66,512]{2,1,0:T(8,128)(2,1)S(1)} %get-tuple-element.6, bf16[4608,512]{1,0:T(8,128)(2,1)} %param.5), kind=kOutput, calls=%fused_computation.29 | convolution fusion | flops 536870912 | bytes 3670016 | tf_op jit(solution)/shard_map/dot_general | solution.py:43
  65.4 3.2 %fusion.18 = f32[16,64,512]{2,1,0:T(8,128)} fusion(bf16[17,66,512]{2,1,0:T(8,128)(2,1)S(1)} %get-tuple-element.6, bf16[4608,512]{1,0:T(8,128)(2,1)} %param.5), kind=kOutput, calls=%fused_computation.31 | convolution fusion | flops 536870912 | bytes 3670016 | tf_op jit(solution)/shard_map/dot_general | solution.py:43
  68.5 3.2 %fusion.24 = f32[16,64,512]{2,1,0:T(8,128)} fusion(bf16[17,66,512]{2,1,0:T(8,128)(2,1)S(1)} %get-tuple-element.5, bf16[4608,512]{1,0:T(8,128)(2,1)} %param.5), kind=kOutput, calls=%fused_computation.39 | convolution fusion | flops 536870912 | bytes 3670016 | tf_op jit(solution)/shard_map/dot_general | solution.py:43
  71.7 86.7 %reduce-scatter.2.cloned.1.call-done = f32[288,512]{1,0:T(8,128)} async-done(((f32[4608,512]{1,0:T(8,128)}), f32[288,512]{1,0:T(8,128)}) %reduce-scatter.2.cloned.1.call-update) | async-done | bytes 589840 | tf_op jit(solution)/shard_map/reduce_scatter | solution.py:83
  158.4 3.6 %fusion.26 = f32[16,64,512]{2,1,0:T(8,128)} fusion(bf16[17,66,512]{2,1,0:T(8,128)(2,1)} %copy-done.2, bf16[4608,512]{1,0:T(8,128)(2,1)} %param.5), kind=kOutput, calls=%fused_computation.41 | convolution fusion | flops 536870912 | bytes 3670016 | tf_op jit(solution)/shard_map/dot_general | solution.py:43
  162.0 3.2 %fusion.28 = f32[16,64,512]{2,1,0:T(8,128)} fusion(bf16[17,66,512]{2,1,0:T(8,128)(2,1)S(1)} %copy-done.3, bf16[4608,512]{1,0:T(8,128)(2,1)} %param.5), kind=kOutput, calls=%fused_computation.43 | convolution fusion | flops 536870912 | bytes 3670016 | tf_op jit(solution)/shard_map/dot_general | solution.py:43
  165.2 25.2 %all-reduce.2.cloned.1.call-done = f32[288,512]{1,0:T(8,128)} async-done(((f32[288,512]{1,0:T(8,128)}), f32[288,512]{1,0:T(8,128)}) %all-reduce.2.cloned.1.call-update) | async-done | bytes 589840 | tf_op jit(solution)/shard_map/psum | solution.py:84
  190.5 1.8 multiply_reduce_fusion
  192.3 7.9 %fusion.2 = bf16[16,64,512]{2,1,0:T(8,128)(2,1)} fusion(bf16[16,64,512]{2,1,0:T(8,128)(2,1)S(1)} %copy-done.5, f32[16,64,512]{2,1,0:T(8,128)} %fusion.16, f32[16,64,512]{2,1,0:T(8,128)} %fusion.18, f32[16,64,512]{2,1,0:T(8,128)} %fusion.20, f32[16,64,512]{2,1,0:T(8,128)S(1)} %fusion.60, f32[16,64,512]{2,1,0:T(8,128)} %fusion.22, f32[16,64,512]{2,1,0:T(8,128)} %fusion.24, ...), kind=kOutput, calls=%fused_computation.4 | convolution fusion | flops 542638080 | bytes 20447232 | tf_op jit(solution)/shard_map/dot_general | solution.py:43
  200.2 33.7 %psum.15 = f32[]{:T(128)} all-reduce(f32[]{:T(128)} %multiply_reduce_fusion), channel_id=1, replica_groups=mesh['lat'=16,'lon'=2] {'lat'}, use_global_device_ids=true, to_apply=%region_3.0 | all-reduce | flops 1 | bytes 8 | tf_op jit(solution)/shard_map/psum | solution.py:85
  234.6 2.3 multiply_add_fusion
  (40 shorter events, 11.4 us)
Async XLA Ops:
  7.2 8.1 %copy-start = (bf16[16,64,512]{2,1,0:T(8,128)(2,1)S(1)}, bf16[16,64,512]{2,1,0:T(8,128)(2,1)}, u32[]{:S(2)}) copy-start(bf16[16,64,512]{2,1,0:T(8,128)(2,1)} %param.3) | copy-start | bytes 3145732
  7.2 151.2 %reduce-scatter.2.cloned.1.call-start = ((), (), s32[]{:S(2)}) async-start(), calls=%async_computation.1 | async-start | bytes 10027008 | tf_op jit(solution)/shard_map/reduce_scatter | solution.py:83
  8.3 5.2 %collective-permute-start = (bf16[16,1,512]{2,1,0:T(2,128)(2,1)S(1)}, bf16[16,1,512]{2,1,0:T(2,128)(2,1)S(1)}, u32[]{:S(2)}, u32[]{:S(2)}) collective-permute-start(bf16[16,1,512]{2,1,0:T(2,128)(2,1)S(1)} %get-tuple-element.15), channel_id=1, source_target_pairs={{0,1},{1,0},{2,3},{3,2},{4,5},{5,4},{6,7},{7,6},{8,9},{9,8},{10,11... | collective-permute-start | bytes 49160 | tf_op jit(solution)/shard_map/ppermute | solution.py:14
  11.4 3.9 %collective-permute-start.1 = (bf16[16,1,512]{2,1,0:T(2,128)(2,1)S(1)}, bf16[16,1,512]{2,1,0:T(2,128)(2,1)S(1)}, u32[]{:S(2)}, u32[]{:S(2)}) collective-permute-start(bf16[16,1,512]{2,1,0:T(2,128)(2,1)S(1)} %get-tuple-element.16), channel_id=1, source_target_pairs={{1,0},{0,1},{3,2},{2,3},{5,4},{4,5},{7,6},{6,7},{9,8},{8,9},{11,10... | collective-permute-start | bytes 49160 | tf_op jit(solution)/shard_map/ppermute | solution.py:17
  15.3 4.7 %copy-start.6 = (bf16[4608,512]{1,0:T(8,128)(2,1)S(1)}, bf16[4608,512]{1,0:T(8,128)(2,1)}, u32[]{:S(2)}) copy-start(bf16[4608,512]{1,0:T(8,128)(2,1)} %param.5) | copy-start | bytes 14155780
  15.3 5.4 %collective-permute-start.2 = (bf16[1,66,512]{2,1,0:T(8,128)(2,1)S(1)}, bf16[1,66,512]{2,1,0:T(8,128)(2,1)S(1)}, u32[]{:S(2)}, u32[]{:S(2)}) collective-permute-start(bf16[1,66,512]{2,1,0:T(8,128)(2,1)S(1)} %get-tuple-element.11), channel_id=1, source_target_pairs={{0,2},{2,4},{4,6},{6,8},{8,10},{10,12},{12,14},{14,16},{16,18},{18... | collective-permute-start | bytes 202760 | tf_op jit(solution)/shard_map/ppermute | solution.py:14
  16.9 4.9 %collective-permute-start.3 = (bf16[1,66,512]{2,1,0:T(8,128)(2,1)S(1)}, bf16[1,66,512]{2,1,0:T(8,128)(2,1)S(1)}, u32[]{:S(2)}, u32[]{:S(2)}) collective-permute-start(bf16[1,66,512]{2,1,0:T(8,128)(2,1)S(1)} %get-tuple-element.12), channel_id=1, source_target_pairs={{2,0},{4,2},{6,4},{8,6},{10,8},{12,10},{14,12},{16,14},{18,16},{20... | collective-permute-start | bytes 202760 | tf_op jit(solution)/shard_map/ppermute | solution.py:17
  25.4 1.2 copy-start.4
  44.2 146.3 %all-reduce.2.cloned.1.call-start = ((), (), s32[]{:S(2)}) async-start(), calls=%async_computation.2 | async-start | bytes 1179648 | tf_op jit(solution)/shard_map/psum | solution.py:84
  44.3 4.0 %collective-permute-start.5 = (bf16[16,1,512]{2,1,0:T(2,128)(2,1)S(1)}, bf16[16,1,512]{2,1,0:T(2,128)(2,1)S(1)}, u32[]{:S(2)}, u32[]{:S(2)}) collective-permute-start(bf16[16,1,512]{2,1,0:T(2,128)(2,1)S(1)} %get-tuple-element.14), channel_id=1, source_target_pairs={{1,0},{0,1},{3,2},{2,3},{5,4},{4,5},{7,6},{6,7},{9,8},{8,9},{11,10... | collective-permute-start | bytes 49160 | tf_op jit(solution)/shard_map/ppermute | solution.py:17
  44.9 3.9 %collective-permute-start.4 = (bf16[16,1,512]{2,1,0:T(2,128)(2,1)S(1)}, bf16[16,1,512]{2,1,0:T(2,128)(2,1)S(1)}, u32[]{:S(2)}, u32[]{:S(2)}) collective-permute-start(bf16[16,1,512]{2,1,0:T(2,128)(2,1)S(1)} %get-tuple-element.13), channel_id=1, source_target_pairs={{0,1},{1,0},{2,3},{3,2},{4,5},{5,4},{6,7},{7,6},{8,9},{9,8},{10,11... | collective-permute-start | bytes 49160 | tf_op jit(solution)/shard_map/ppermute | solution.py:14
  48.8 12.2 %collective-permute-start.6 = (bf16[1,66,512]{2,1,0:T(8,128)(2,1)S(1)}, bf16[1,66,512]{2,1,0:T(8,128)(2,1)S(1)}, u32[]{:S(2)}, u32[]{:S(2)}) collective-permute-start(bf16[1,66,512]{2,1,0:T(8,128)(2,1)S(1)} %get-tuple-element.7), channel_id=1, source_target_pairs={{2,0},{4,2},{6,4},{8,6},{10,8},{12,10},{14,12},{16,14},{18,16},{20... | collective-permute-start | bytes 202760 | tf_op jit(solution)/shard_map/ppermute | solution.py:17
  50.1 10.9 %collective-permute-start.7 = (bf16[1,66,512]{2,1,0:T(8,128)(2,1)S(1)}, bf16[1,66,512]{2,1,0:T(8,128)(2,1)S(1)}, u32[]{:S(2)}, u32[]{:S(2)}) collective-permute-start(bf16[1,66,512]{2,1,0:T(8,128)(2,1)S(1)} %get-tuple-element.8), channel_id=1, source_target_pairs={{0,2},{2,4},{4,6},{6,8},{8,10},{10,12},{12,14},{14,16},{16,18},{18... | collective-permute-start | bytes 202760 | tf_op jit(solution)/shard_map/ppermute | solution.py:14
  61.8 6.8 %copy-start.1 = (bf16[17,66,512]{2,1,0:T(8,128)(2,1)}, bf16[17,66,512]{2,1,0:T(8,128)(2,1)S(1)}, u32[]{:S(2)}) copy-start(bf16[17,66,512]{2,1,0:T(8,128)(2,1)S(1)} %get-tuple-element.6) | copy-start | bytes 3446788
  61.8 6.8 %copy-start.2 = (bf16[17,66,512]{2,1,0:T(8,128)(2,1)}, bf16[17,66,512]{2,1,0:T(8,128)(2,1)S(1)}, u32[]{:S(2)}) copy-start(bf16[17,66,512]{2,1,0:T(8,128)(2,1)S(1)} %get-tuple-element.5) | copy-start | bytes 3446788
  158.4 3.6 %copy-start.3 = (bf16[17,66,512]{2,1,0:T(8,128)(2,1)S(1)}, bf16[17,66,512]{2,1,0:T(8,128)(2,1)}, u32[]{:S(2)}) copy-start(bf16[17,66,512]{2,1,0:T(8,128)(2,1)} %copy-done.2) | copy-start | bytes 3446788
  162.0 30.3 %copy-start.5 = (bf16[16,64,512]{2,1,0:T(8,128)(2,1)S(1)}, bf16[16,64,512]{2,1,0:T(8,128)(2,1)}, u32[]{:S(2)}) copy-start(bf16[16,64,512]{2,1,0:T(8,128)(2,1)} %param.4) | copy-start | bytes 3145732
Sparse Core Ops, SparseCore 0:
  44.3 114.0 reduce-scatter.1
  160.7 29.7 all-reduce.1
where the time goes:
time: 244 us
  waiting for transfers between devices  115 us (47%)
  matrix products  58.5 us (24%)
  blocking collectives  33.7 us (14%)
  between operations  14.9 us (6%)
  starting transfers between devices  13.8 us (6%)
  other arithmetic  5.77 us (2%)
    reduce_scatter x1, waiting for transfers between devices, shards(): lax.psum_scatter(local_grad, 'lat', scatter_dimension=0, tiled=True)  86.7 us
    psum x1, blocking collectives, shards(): total = lax.psum(jnp.sum(summed * summed), 'lat')  33.7 us
    dot_general x9, matrix products, spread(): lax.dot_general(piece, kernel[t * channels:(t + 1) * channels], (((2,), (...  32.9 us
    psum x1, waiting for transfers between devices, shards(): summed = lax.psum(row_block, 'lon')  25.2 us
    dot_general x9, matrix products, weight_terms(): lax.dot_general(padded[a:a + height, b:b + breadth], slope, (((0, 1), (0,...  15.7 us
    ppermute x4, starting transfers between devices, padded_2(): lax.ppermute(lax.slice_in_dim(block, block.shape[dim] - width, None, axis...  10.5 us
    dot_general x9, matrix products, convolve(): jnp.dot(padded[a:a + height, b:b + breadth], kernel[t * channels:(t + 1)...  9.83 us
  transfers between devices with their start and end apart: 10, of which 6 were waited for; matrix products, arithmetic and copies ran while one was open for 12% of the time, Pallas kernels for 0%

commit v1 on v0

--- a/solution.py
+++ b/solution.py
@@ -81,7 +81,7 @@
     input_grad = back.astype(jnp.bfloat16)
     local_grad = weight_terms(padded_x, slope, height, breadth)
     row_block = lax.psum_scatter(local_grad, "lat", scatter_dimension=0, tiled=True)
-    summed = lax.psum(row_block, "lon")
+    summed = jax.lax.all_gather(row_block, axis_name="lon").sum(axis=0)
     total = lax.psum(jnp.sum(summed * summed), "lat")
     count = 9.0 * channels * channels
     direction = summed / jnp.sqrt(total / count + 1e-06)

time: 244 us -> 237 us (0.971)
  waiting for transfers between devices: 115 us -> 106 us
    psum x1 -> x0, waiting for transfers between devices: 25.2 us -> none  [shards(): summed = lax.psum(row_block, 'lon')]
    all_gather x0 -> x1, waiting for transfers between devices: none -> 11 us  [shards(): summed = jax.lax.all_gather(row_block, axis_name='lon').sum(axis=0)]
    reduce_scatter x1, waiting for transfers between devices: 86.7 us -> 91.4 us  [shards(): lax.psum_scatter(local_grad, 'lat', scatter_dimension=0, tiled=True)]
  transfers between devices with their start and end apart: 10 -> 10, of which waited for: 6 -> 6; matrix products, arithmetic and copies ran while one was open for 12% -> 13% of each run, Pallas kernels for 0% -> 0%
where the time goes in v1:
time: 237 us; the launch traced here: 236 us
  waiting for transfers between devices  106 us (45%)
  matrix products  58.2 us (25%)
  blocking collectives  33.7 us (14%)
  between operations  14.9 us (6%)
  starting transfers between devices  13.8 us (6%)
  other arithmetic  6.97 us (3%)
  local copies, waits for them, and re-layouts  2.74 us (1%)
    reduce_scatter x1, waiting for transfers between devices, shards(): lax.psum_scatter(local_grad, 'lat', scatter_dimension=0, tiled=True)  91.4 us
    psum x1, blocking collectives, shards(): total = lax.psum(jnp.sum(summed * summed), 'lat')  33.7 us
    dot_general x9, matrix products, spread(): lax.dot_general(piece, kernel[t * channels:(t + 1) * channels], (((2,), (...  32.6 us
    dot_general x9, matrix products, weight_terms(): lax.dot_general(padded[a:a + height, b:b + breadth], slope, (((0, 1), (0,...  15.7 us
    all_gather x1, waiting for transfers between devices, shards(): summed = jax.lax.all_gather(row_block, axis_name='lon').sum(axis=0)  11 us
    ppermute x4, starting transfers between devices, padded_2(): lax.ppermute(lax.slice_in_dim(block, block.shape[dim] - width, None, axis...  10.5 us
    dot_general x9, matrix products, convolve(): jnp.dot(padded[a:a + height, b:b + breadth], kernel[t * channels:(t + 1)...  9.83 us
  transfers between devices with their start and end apart: 10, of which 6 were waited for; matrix products, arithmetic and copies ran while one was open for 13% of the time, Pallas kernels for 0%

profile of v1, /device:TPU:0, one launch (start us, length us, event | category | flops | bytes accessed | tf_op | source)
XLA Modules:
  0.0 236.1 jit_solution(14578723590189154538)
XLA Ops:
  8.3 3.0 %collective-permute-start = (bf16[16,1,512]{2,1,0:T(2,128)(2,1)S(1)}, bf16[16,1,512]{2,1,0:T(2,128)(2,1)S(1)}, u32[]{:S(2)}, u32[]{:S(2)}) collective-permute-start(bf16[16,1,512]{2,1,0:T(2,128)(2,1)S(1)} %get-tuple-element.15), channel_id=1, source_target_pairs={{0,1},{1,0},{2,3},{3,2},{4,5},{5,4},{6,7},{7,6},{8,9},{9,8},{10,11... | collective-permute-start | bytes 49160 | tf_op jit(solution)/shard_map/ppermute | solution.py:14
  11.4 2.1 fusion.62
  13.5 1.8 collective-permute-done.1
  15.3 1.6 collective-permute-start.2
  18.2 1.8 fusion.50
  26.6 1.8 fusion.1
  28.4 1.7 fusion.11
  30.1 1.7 fusion.10
  31.9 1.7 fusion.9
  33.6 1.7 fusion.8
  35.3 1.7 fusion.7
  37.0 1.8 fusion.6
  38.8 1.7 fusion.5
  40.5 1.8 fusion.4
  42.3 1.8 fusion.3
  44.8 1.5 collective-permute-start.4
  46.3 1.8 fusion.60
  50.1 4.4 %collective-permute-start.7 = (bf16[1,66,512]{2,1,0:T(8,128)(2,1)S(1)}, bf16[1,66,512]{2,1,0:T(8,128)(2,1)S(1)}, u32[]{:S(2)}, u32[]{:S(2)}) collective-permute-start(bf16[1,66,512]{2,1,0:T(8,128)(2,1)S(1)} %get-tuple-element.8), channel_id=1, source_target_pairs={{0,2},{2,4},{4,6},{6,8},{8,10},{10,12},{12,14},{14,16},{16,18},{18... | collective-permute-start | bytes 202760 | tf_op jit(solution)/shard_map/ppermute | solution.py:14
  54.5 3.3 %fusion.22 = f32[16,64,512]{2,1,0:T(8,128)} fusion(bf16[16,1,512]{2,1,0:T(2,128)(2,1)S(1)} %collective-permute-done.5, bf16[16,64,512]{2,1,0:T(8,128)(2,1)S(1)} %fusion.1, bf16[4608,512]{1,0:T(8,128)(2,1)} %param.5), kind=kOutput, calls=%fused_computation.37 | convolution fusion | flops 538968064 | bytes 3686400 | tf_op jit(solution)/shard_map/dot_general | solution.py:43
  57.8 3.1 %fusion.20 = f32[16,64,512]{2,1,0:T(8,128)} fusion(bf16[16,64,512]{2,1,0:T(8,128)(2,1)S(1)} %fusion.1, bf16[16,1,512]{2,1,0:T(2,128)(2,1)S(1)} %collective-permute-done.4, bf16[4608,512]{1,0:T(8,128)(2,1)} %param.5), kind=kOutput, calls=%fused_computation.34 | convolution fusion | flops 538968064 | bytes 3686400 | tf_op jit(solution)/shard_map/dot_general | solution.py:43
  61.0 1.8 pad_maximum_fusion.1
  63.8 3.2 %fusion.16 = f32[16,64,512]{2,1,0:T(8,128)} fusion(bf16[17,66,512]{2,1,0:T(8,128)(2,1)S(1)} %get-tuple-element.6, bf16[4608,512]{1,0:T(8,128)(2,1)} %param.5), kind=kOutput, calls=%fused_computation.29 | convolution fusion | flops 536870912 | bytes 3670016 | tf_op jit(solution)/shard_map/dot_general | solution.py:43
  67.0 91.4 %reduce-scatter.2.cloned.1.call-done = f32[288,512]{1,0:T(8,128)} async-done(((f32[4608,512]{1,0:T(8,128)}), f32[288,512]{1,0:T(8,128)}) %reduce-scatter.2.cloned.1.call-update) | async-done | bytes 589840 | tf_op jit(solution)/shard_map/reduce_scatter | solution.py:83
  158.4 3.6 %fusion.18 = f32[16,64,512]{2,1,0:T(8,128)} fusion(bf16[17,66,512]{2,1,0:T(8,128)(2,1)} %copy-done.1, bf16[4608,512]{1,0:T(8,128)(2,1)} %param.5), kind=kOutput, calls=%fused_computation.31 | convolution fusion | flops 536870912 | bytes 3670016 | tf_op jit(solution)/shard_map/dot_general | solution.py:43
  162.0 3.1 %fusion.24 = f32[16,64,512]{2,1,0:T(8,128)} fusion(bf16[17,66,512]{2,1,0:T(8,128)(2,1)S(1)} %copy-done.2, bf16[4608,512]{1,0:T(8,128)(2,1)} %param.5), kind=kOutput, calls=%fused_computation.39 | convolution fusion | flops 536870912 | bytes 3670016 | tf_op jit(solution)/shard_map/dot_general | solution.py:43
  165.1 3.2 %fusion.26 = f32[16,64,512]{2,1,0:T(8,128)} fusion(bf16[17,66,512]{2,1,0:T(8,128)(2,1)S(1)} %copy-done.2, bf16[4608,512]{1,0:T(8,128)(2,1)} %param.5), kind=kOutput, calls=%fused_computation.41 | convolution fusion | flops 536870912 | bytes 3670016 | tf_op jit(solution)/shard_map/dot_general | solution.py:43
  168.3 3.1 %fusion.28 = f32[16,64,512]{2,1,0:T(8,128)} fusion(bf16[17,66,512]{2,1,0:T(8,128)(2,1)S(1)} %copy-done.2, bf16[4608,512]{1,0:T(8,128)(2,1)} %param.5), kind=kOutput, calls=%fused_computation.43 | convolution fusion | flops 536870912 | bytes 3670016 | tf_op jit(solution)/shard_map/dot_general | solution.py:43
  171.4 11.0 %all-gather.3.cloned.1.call-done = f32[576,512]{1,0:T(8,128)} async-done(((f32[288,512]{1,0:T(8,128)}), f32[576,512]{1,0:T(8,128)}) %all-gather.3.cloned.1.call-update) | async-done | bytes 1179664 | tf_op jit(solution)/shard_map/all_gather | solution.py:84
  182.3 1.4 reduce_sum.18
  184.5 8.2 %fusion.2 = bf16[16,64,512]{2,1,0:T(8,128)(2,1)} fusion(bf16[16,64,512]{2,1,0:T(8,128)(2,1)} %param.4, f32[16,64,512]{2,1,0:T(8,128)} %fusion.16, f32[16,64,512]{2,1,0:T(8,128)} %fusion.18, f32[16,64,512]{2,1,0:T(8,128)} %fusion.20, f32[16,64,512]{2,1,0:T(8,128)S(1)} %fusion.60, f32[16,64,512]{2,1,0:T(8,128)} %fusion.22, f32[16,64,512]{2,1,0:T(8,128)} %fusion.24, ...), kind=kOutput, calls=%fused_computation.4 | convolution fusion | flops 542638080 | bytes 20447232 | tf_op jit(solution)/shard_map/dot_general | solution.py:43
  192.7 33.7 %psum.7 = f32[]{:T(128)} all-reduce(f32[]{:T(128)} %multiply_reduce_fusion), channel_id=1, replica_groups=mesh['lat'=16,'lon'=2] {'lat'}, use_global_device_ids=true, to_apply=%region_3.0 | all-reduce | flops 1 | bytes 8 | tf_op jit(solution)/shard_map/psum | solution.py:85
  227.1 2.2 multiply_add_fusion
  (37 shorter events, 13.7 us)
Async XLA Ops:
  7.2 8.1 %copy-start = (bf16[16,64,512]{2,1,0:T(8,128)(2,1)S(1)}, bf16[16,64,512]{2,1,0:T(8,128)(2,1)}, u32[]{:S(2)}) copy-start(bf16[16,64,512]{2,1,0:T(8,128)(2,1)} %param.3) | copy-start | bytes 3145732
  7.2 151.2 %reduce-scatter.2.cloned.1.call-start = ((), (), s32[]{:S(2)}) async-start(), calls=%async_computation.1 | async-start | bytes 10027008 | tf_op jit(solution)/shard_map/reduce_scatter | solution.py:83
  8.3 5.2 %collective-permute-start = (bf16[16,1,512]{2,1,0:T(2,128)(2,1)S(1)}, bf16[16,1,512]{2,1,0:T(2,128)(2,1)S(1)}, u32[]{:S(2)}, u32[]{:S(2)}) collective-permute-start(bf16[16,1,512]{2,1,0:T(2,128)(2,1)S(1)} %get-tuple-element.15), channel_id=1, source_target_pairs={{0,1},{1,0},{2,3},{3,2},{4,5},{5,4},{6,7},{7,6},{8,9},{9,8},{10,11... | collective-permute-start | bytes 49160 | tf_op jit(solution)/shard_map/ppermute | solution.py:14
  11.4 3.9 %collective-permute-start.1 = (bf16[16,1,512]{2,1,0:T(2,128)(2,1)S(1)}, bf16[16,1,512]{2,1,0:T(2,128)(2,1)S(1)}, u32[]{:S(2)}, u32[]{:S(2)}) collective-permute-start(bf16[16,1,512]{2,1,0:T(2,128)(2,1)S(1)} %get-tuple-element.16), channel_id=1, source_target_pairs={{1,0},{0,1},{3,2},{2,3},{5,4},{4,5},{7,6},{6,7},{9,8},{8,9},{11,10... | collective-permute-start | bytes 49160 | tf_op jit(solution)/shard_map/ppermute | solution.py:17
  15.3 4.7 %copy-start.4 = (bf16[4608,512]{1,0:T(8,128)(2,1)S(1)}, bf16[4608,512]{1,0:T(8,128)(2,1)}, u32[]{:S(2)}) copy-start(bf16[4608,512]{1,0:T(8,128)(2,1)} %param.5) | copy-start | bytes 14155780
  15.3 5.4 %collective-permute-start.2 = (bf16[1,66,512]{2,1,0:T(8,128)(2,1)S(1)}, bf16[1,66,512]{2,1,0:T(8,128)(2,1)S(1)}, u32[]{:S(2)}, u32[]{:S(2)}) collective-permute-start(bf16[1,66,512]{2,1,0:T(8,128)(2,1)S(1)} %get-tuple-element.11), channel_id=1, source_target_pairs={{0,2},{2,4},{4,6},{6,8},{8,10},{10,12},{12,14},{14,16},{16,18},{18... | collective-permute-start | bytes 202760 | tf_op jit(solution)/shard_map/ppermute | solution.py:14
  16.9 4.9 %collective-permute-start.3 = (bf16[1,66,512]{2,1,0:T(8,128)(2,1)S(1)}, bf16[1,66,512]{2,1,0:T(8,128)(2,1)S(1)}, u32[]{:S(2)}, u32[]{:S(2)}) collective-permute-start(bf16[1,66,512]{2,1,0:T(8,128)(2,1)S(1)} %get-tuple-element.12), channel_id=1, source_target_pairs={{2,0},{4,2},{6,4},{8,6},{10,8},{12,10},{14,12},{16,14},{18,16},{20... | collective-permute-start | bytes 202760 | tf_op jit(solution)/shard_map/ppermute | solution.py:17
  25.4 1.2 copy-start.3
  44.1 138.2 %all-gather.3.cloned.1.call-start = ((), (), s32[]{:S(2)}) async-start(), calls=%async_computation.2 | async-start | bytes 1769472 | tf_op jit(solution)/shard_map/all_gather | solution.py:84
  44.2 4.0 %collective-permute-start.5 = (bf16[16,1,512]{2,1,0:T(2,128)(2,1)S(1)}, bf16[16,1,512]{2,1,0:T(2,128)(2,1)S(1)}, u32[]{:S(2)}, u32[]{:S(2)}) collective-permute-start(bf16[16,1,512]{2,1,0:T(2,128)(2,1)S(1)} %get-tuple-element.14), channel_id=1, source_target_pairs={{1,0},{0,1},{3,2},{2,3},{5,4},{4,5},{7,6},{6,7},{9,8},{8,9},{11,10... | collective-permute-start | bytes 49160 | tf_op jit(solution)/shard_map/ppermute | solution.py:17
  44.8 3.9 %collective-permute-start.4 = (bf16[16,1,512]{2,1,0:T(2,128)(2,1)S(1)}, bf16[16,1,512]{2,1,0:T(2,128)(2,1)S(1)}, u32[]{:S(2)}, u32[]{:S(2)}) collective-permute-start(bf16[16,1,512]{2,1,0:T(2,128)(2,1)S(1)} %get-tuple-element.13), channel_id=1, source_target_pairs={{0,1},{1,0},{2,3},{3,2},{4,5},{5,4},{6,7},{7,6},{8,9},{9,8},{10,11... | collective-permute-start | bytes 49160 | tf_op jit(solution)/shard_map/ppermute | solution.py:14
  48.8 12.2 %collective-permute-start.6 = (bf16[1,66,512]{2,1,0:T(8,128)(2,1)S(1)}, bf16[1,66,512]{2,1,0:T(8,128)(2,1)S(1)}, u32[]{:S(2)}, u32[]{:S(2)}) collective-permute-start(bf16[1,66,512]{2,1,0:T(8,128)(2,1)S(1)} %get-tuple-element.7), channel_id=1, source_target_pairs={{2,0},{4,2},{6,4},{8,6},{10,8},{12,10},{14,12},{16,14},{18,16},{20... | collective-permute-start | bytes 202760 | tf_op jit(solution)/shard_map/ppermute | solution.py:17
  50.1 10.9 %collective-permute-start.7 = (bf16[1,66,512]{2,1,0:T(8,128)(2,1)S(1)}, bf16[1,66,512]{2,1,0:T(8,128)(2,1)S(1)}, u32[]{:S(2)}, u32[]{:S(2)}) collective-permute-start(bf16[1,66,512]{2,1,0:T(8,128)(2,1)S(1)} %get-tuple-element.8), channel_id=1, source_target_pairs={{0,2},{2,4},{4,6},{6,8},{8,10},{10,12},{12,14},{14,16},{16,18},{18... | collective-permute-start | bytes 202760 | tf_op jit(solution)/shard_map/ppermute | solution.py:14
  62.8 1.1 copy-start.1
  158.4 3.6 %copy-start.2 = (bf16[17,66,512]{2,1,0:T(8,128)(2,1)S(1)}, bf16[17,66,512]{2,1,0:T(8,128)(2,1)}, u32[]{:S(2)}) copy-start(bf16[17,66,512]{2,1,0:T(8,128)(2,1)} %get-tuple-element.5) | copy-start | bytes 3446788
Sparse Core Ops, SparseCore 0:
  44.3 114.0 reduce-scatter.1
  159.9 22.3 all-gather.2
